TPU v7x, 32 devices: a whole 2x2x4 slice. The times are simulated.
32 devices in a mesh: dp: 4 (over x, core), expert: 4 (over z), etp: 2 (over y).
Axes of the slice: x: 2, y: 2, z: 4, core: 2. Of those that a mesh axis runs over, the one named last changes fastest.
Arguments:
- tokens: bfloat16 [4096, 3072], P(('dp', 'expert'), 'etp'), parts along dimension 0, may hold values from -6 to 6
- experts: int32 [4096, 2], P(('dp', 'expert')), parts along dimension 0, may hold values from 0 to 3, all different within a row; in each aligned block of 256 rows (0 to 255, 256 to 511, ...) at most 176 rows name the same one
- mixing: float32 [4096, 2], P(('dp', 'expert')), parts along dimension 0, may hold values from 0.2 to 1
- up_weight: bfloat16 [4, 3072, 8192], P('expert', None, 'etp'), may hold values from -0.109375 to 0.109375
- down_weight: bfloat16 [4, 8192, 3072], P('expert', 'etp'), may hold values from -0.0625 to 0.0625
Outputs:
- mixed: bfloat16 [4096, 3072], P(('dp', 'expert'), 'etp'), parts along dimension 0
There are 4 independent parts, one for each index of `dp`. A program takes and returns all parts, laid end to end along the dimension named above; an argument that names none is the same for every part. Nothing has to cross between parts.
Inputs may be any that keep to these rules, and one draw needn't show every extreme that they name: Each row names two different experts. In the rows of one index of expert (aligned blocks of 256 rows) no expert is named more than 176 times, a bound that some block reaches.
All inputs are finite; a program needn't handle non-finite values.
Results may differ from a plain program's by a relative error of at most 0.0078.
Values may be sent and summed in bfloat16 or wider, within the bound.
A program may use at most 128 MiB of HBM per device.

v0:
```python
import jax
import jax.numpy as jnp
from jax import lax
from jax.sharding import PartitionSpec as P


def slot_table(chosen, expert_count, capacity):
    flat_ids = chosen.reshape(-1)
    one_hot = (flat_ids[:, None] == jnp.arange(expert_count, dtype=jnp.int32)[None, :]).astype(
        jnp.int32
    )
    before = jnp.cumsum(one_hot, axis=0) - one_hot
    position = jnp.sum(before * one_hot, axis=1)
    return (flat_ids * capacity + position).reshape(chosen.shape)


def dispatch_rows(block_tokens, slot_ids, slot_total):
    one_hot = (
        slot_ids[:, :, None] == jnp.arange(slot_total, dtype=jnp.int32)[None, None, :]
    ).astype(jnp.bfloat16)
    placing = jnp.sum(one_hot, axis=1)
    return jnp.einsum(
        "rs,rd->sd", placing, block_tokens, preferred_element_type=jnp.float32
    ).astype(jnp.bfloat16)


def local(tokens, experts, mixing, up_weight, down_weight):
    tok_rows = experts.shape[0]
    part_width = tokens.shape[1]
    expert_count = up_weight.shape[0] * lax.axis_size("expert")
    capacity = 2 * tok_rows // expert_count * 11 // 8
    slot_total = expert_count * capacity
    up_slab = up_weight[0]
    down_slab = down_weight[0]
    slot_ids = slot_table(experts, expert_count, capacity)
    outgoing = dispatch_rows(tokens, slot_ids, slot_total).reshape(
        expert_count, capacity, part_width
    )
    arrived = lax.all_to_all(outgoing, "expert", split_axis=0, concat_axis=0, tiled=True)
    gathered = lax.all_gather(arrived.reshape(slot_total, part_width), "etp", axis=1, tiled=True)
    up_proj = jnp.dot(gathered, up_slab, preferred_element_type=jnp.float32)
    hidden = jax.nn.silu(up_proj).astype(jnp.bfloat16)
    partial_sums = jnp.dot(hidden, down_slab, preferred_element_type=jnp.float32)
    own_cols = lax.psum_scatter(partial_sums, "etp", scatter_dimension=1, tiled=True).astype(
        jnp.bfloat16
    )
    outputs = lax.all_to_all(
        own_cols.reshape(expert_count, capacity, part_width),
        "expert",
        split_axis=0,
        concat_axis=0,
        tiled=True,
    )
    flat_out = outputs.reshape(slot_total, part_width)
    picked = (
        jnp.take(flat_out, slot_ids.reshape(-1), axis=0)
        .reshape(tok_rows, 2, part_width)
        .astype(jnp.float32)
    )
    mixed = jnp.sum(picked * mixing[:, :, None], axis=1)
    return mixed.astype(jnp.bfloat16)


def solution(mesh):
    placed = (
        P(("dp", "expert"), "etp"),
        P(("dp", "expert"), None),
        P(("dp", "expert"), None),
        P("expert", None, "etp"),
        P("expert", "etp", None),
    )
    return jax.shard_map(
        local, mesh=mesh, in_specs=placed, out_specs=P(("dp", "expert"), "etp"), check_vma=False
    )
```

profile of v0, /device:TPU:0, one launch (start us, length us, event | category | flops | bytes accessed | tf_op | source)
XLA Modules:
  0.0 352.5 jit_solution(7086791842899878181)
XLA Ops:
  6.5 0.9 copy.18
  7.4 0.1 eq.39
  7.6 0.1 reshape.81
  7.7 1.2 reduce-window.6
  9.0 0.2 slice_reduce_fusion
  9.2 0.2 reduce-window.9
  9.5 0.1 reduce_sum.35
  9.7 0.7 compare_and_fusion
  10.4 0.3 fusion.10
  10.7 0.7 convolution_convert_fusion
  11.4 55.9 %all_to_all.10 = bf16[4,176,1536]{2,1,0:T(8,128)(2,1)} all-to-all(bf16[4,176,1536]{2,1,0:T(8,128)(2,1)S(1)} %bitcast.47), channel_id=1, replica_groups=mesh['dp'=4,'expert'=4,'etp'=2] {'expert'}, dimensions={0} | all-to-all | bytes 4325376 | tf_op jit(solution)/shard_map/all_to_all | solution.py:39
  67.4 57.5 %all-gather.2.cloned.1.call-done = bf16[704,3072]{1,0:T(8,128)(2,1)} async-done(((bf16[704,1536]{1,0:T(8,128)(2,1)}), bf16[704,3072]{1,0:T(8,128)(2,1)}) %all-gather.2.cloned.1.call-update) | async-done | bytes 4325392 | tf_op jit(solution)/shard_map/all_gather | solution.py:40
  124.9 23.9 %multiply_convert_fusion.4 = bf16[704,4096]{1,0:T(8,128)(2,1)S(1)} fusion(bf16[704,3072]{1,0:T(8,128)(2,1)} %all-gather.2.cloned.1.call-done, bf16[1,3072,4096]{2,1,0:T(8,128)(2,1)} %param.8), kind=kOutput, calls=%fused_computation.5.clone.clone.1 | convolution fusion | flops 17731158016 | bytes 35258368 | tf_op jit(solution)/shard_map/dot_general | solution.py:41
  148.8 22.8 %fusion = f32[704,3072]{1,0:T(8,128)} fusion(bf16[1,4096,3072]{2,1,0:T(8,128)(2,1)} %param.9, bf16[704,4096]{1,0:T(8,128)(2,1)S(1)} %multiply_convert_fusion.4), kind=kOutput, calls=%fused_computation.1 | convolution fusion | flops 17716740096 | bytes 39583744 | tf_op jit(solution)/shard_map/dot_general | solution.py:43
  171.6 102.3 %reduce-scatter.2.cloned.1.call-done = f32[704,1536]{1,0:T(8,128)} async-done(((f32[704,3072]{1,0:T(8,128)}), f32[704,1536]{1,0:T(8,128)}) %reduce-scatter.2.cloned.1.call-update) | async-done | bytes 4325392 | tf_op jit(solution)/shard_map/reduce_scatter | solution.py:44
  273.9 3.8 %convert_element_type.32 = bf16[704,1536]{1,0:T(8,128)(2,1)} convert(f32[704,1536]{1,0:T(8,128)} %reduce-scatter.2.cloned.1.call-done) | non-fusion elementwise | flops 1081344 | bytes 6488064 | tf_op jit(solution)/shard_map/convert_element_type | solution.py:44
  277.7 4.6 %all-to-all-start.1 = ((bf16[4,176,1536]{2,1,0:T(8,128)(2,1)}), bf16[4,176,1536]{2,1,0:T(8,128)(2,1)S(1)}, u32[]{:S(2)}, u32[]{:S(2)}) async-start(bf16[4,176,1536]{2,1,0:T(8,128)(2,1)} %bitcast.48), calls=%async_computation.2 | async-start | bytes 4325376 | tf_op jit(solution)/shard_map/all_to_all | solution.py:47
  282.4 0.1 copy.22
  282.5 0.1 mul.40
  282.7 0.2 copy.21
  283.0 48.8 %all-to-all-done.1 = bf16[4,176,1536]{2,1,0:T(8,128)(2,1)S(1)} async-done(((bf16[4,176,1536]{2,1,0:T(8,128)(2,1)}), bf16[4,176,1536]{2,1,0:T(8,128)(2,1)S(1)}, u32[]{:S(2)}, u32[]{:S(2)}) %all-to-all-start.1) | async-done | bytes 2162720 | tf_op jit(solution)/shard_map/all_to_all | solution.py:47
  331.8 3.0 gather_fusion
  334.8 3.5 gather.7
  338.3 7.4 %multiply_reduce_fusion = bf16[256,1536]{1,0:T(8,128)(2,1)} fusion(bf16[256,2,1536]{2,1,0:T(2,128)(2,1)S(1)} %gather.7, pred[256,2]{1,0:T(8,128)(4,1)S(1)} %copy.21, f32[256,2]{1,0:T(8,128)S(1)} %copy.23), kind=kLoop, calls=%fused_computation.8 | loop fusion | flops 2752512 | bytes 2361856 | tf_op jit(solution)/shard_map/reduce_sum | solution.py:60
  (20 shorter events, 0.4 us)
Async XLA Ops:
  6.5 4.2 %copy-start = (bf16[256,1536]{1,0:T(8,128)(2,1)S(1)}, bf16[256,1536]{1,0:T(8,128)(2,1)}, u32[]{:S(2)}) copy-start(bf16[256,1536]{1,0:T(8,128)(2,1)} %param.5) | copy-start | bytes 2359300
  6.5 118.4 %all-gather.2.cloned.1.call-start = ((), (), s32[]{:S(2)}) async-start(), calls=%async_computation.3 | async-start | bytes 6488064 | tf_op jit(solution)/shard_map/all_gather | solution.py:40
  67.3 206.6 %reduce-scatter.2.cloned.1.call-start = ((), (), s32[]{:S(2)}) async-start(), calls=%async_computation.4 | async-start | bytes 12976128 | tf_op jit(solution)/shard_map/reduce_scatter | solution.py:44
  171.6 110.7 %copy-start.2 = (s32[256,2]{0,1:T(2,128)S(1)}, s32[256,2]{0,1:T(2,128)}, u32[]{:S(2)}) copy-start(s32[256,2]{0,1:T(2,128)} %param.6) | copy-start | bytes 6148
  171.6 111.2 %copy-start.3 = (f32[256,2]{0,1:T(2,128)S(1)}, f32[256,2]{0,1:T(2,128)}, u32[]{:S(2)}) copy-start(f32[256,2]{0,1:T(2,128)} %param.7) | copy-start | bytes 6148
  277.7 54.1 %all-to-all-start.1 = ((bf16[4,176,1536]{2,1,0:T(8,128)(2,1)}), bf16[4,176,1536]{2,1,0:T(8,128)(2,1)S(1)}, u32[]{:S(2)}, u32[]{:S(2)}) async-start(bf16[4,176,1536]{2,1,0:T(8,128)(2,1)} %bitcast.48), calls=%async_computation.2 | async-start | bytes 4325376 | tf_op jit(solution)/shard_map/all_to_all | solution.py:47
  331.8 13.9 %copy-start.1 = (bf16[256,1536]{1,0:T(8,128)(2,1)S(1)}, bf16[256,1536]{1,0:T(8,128)(2,1)}, u32[]{:S(2)}) copy-start(bf16[256,1536]{1,0:T(8,128)(2,1)} %param.5) | copy-start | bytes 2359300
Sparse Core Ops, SparseCore 0:
  67.4 57.4 all-gather.1
  171.7 102.1 reduce-scatter.1
where the time goes:
time: 353 us
  waiting for transfers between devices  209 us (59%)
  blocking collectives  55.9 us (16%)
  matrix products  47.4 us (13%)
  other arithmetic  13.8 us (4%)
  between operations  13.5 us (4%)
  local copies, waits for them, and re-layouts  8.66 us (2%)
  starting transfers between devices  4.67 us (1%)
    reduce_scatter x1, waiting for transfers between devices, local(): lax.psum_scatter(partial_sums, 'etp', scatter_dimension=1, tiled=True)  102 us
    all_gather x1, waiting for transfers between devices, local(): lax.all_gather(arrived.reshape(slot_total, part_width), 'etp', axis=1, ti...  57.5 us
    all_to_all x1, blocking collectives, local(): lax.all_to_all(outgoing, 'expert', split_axis=0, concat_axis=0, tiled=True)  55.9 us
    all_to_all x1, waiting for transfers between devices, local(): lax.all_to_all(own_cols.reshape(expert_count, capacity, part_width), 'exp...  48.8 us
    dot_general x1, matrix products, local(): up_proj = jnp.dot(gathered, up_slab, preferred_element_type=jnp.float32)  23.9 us
    dot_general x1, matrix products, local(): jnp.dot(hidden, down_slab, preferred_element_type=jnp.float32)  22.8 us
    reduce_sum x1, other arithmetic, local(): mixed = jnp.sum(picked * mixing[:, :, None], axis=1)  7.44 us
  transfers between devices with their start and end apart: 3, of which 3 were waited for; matrix products, arithmetic and copies ran while one was open for 0% of the time, Pallas kernels for 0%

commit v1 on v0

--- a/solution.py
+++ b/solution.py
@@ -2,6 +2,18 @@
 import jax.numpy as jnp
 from jax import lax
 from jax.sharding import PartitionSpec as P
+
+
+def collect(x, axis, dim):
+    ways, here, step = (lax.axis_size(axis), lax.axis_index(axis), x.shape[dim])
+    line, have = (x, 1)
+    while have < ways:
+        line = jnp.concatenate(
+            [line, lax.ppermute(line, axis, [(d, (d - have) % ways) for d in range(ways)])],
+            axis=dim,
+        )
+        have = 2 * have
+    return jnp.roll(line, here * step, axis=dim)
 
 
 def slot_table(chosen, expert_count, capacity):
@@ -37,7 +49,7 @@
         expert_count, capacity, part_width
     )
     arrived = lax.all_to_all(outgoing, "expert", split_axis=0, concat_axis=0, tiled=True)
-    gathered = lax.all_gather(arrived.reshape(slot_total, part_width), "etp", axis=1, tiled=True)
+    gathered = collect(arrived.reshape(slot_total, part_width), "etp", 1)
     up_proj = jnp.dot(gathered, up_slab, preferred_element_type=jnp.float32)
     hidden = jax.nn.silu(up_proj).astype(jnp.bfloat16)
     partial_sums = jnp.dot(hidden, down_slab, preferred_element_type=jnp.float32)

time: 353 us -> 353 us (level)
  waiting for transfers between devices: 209 us -> 197 us
  matrix products: 47.4 us -> 57.7 us
    all_gather x1 -> x0, waiting for transfers between devices: 57.5 us -> none  [local(): lax.all_gather(arrived.reshape(slot_total, part_width), 'etp', axis=1, ti...]
    ppermute x0 -> x1, waiting for transfers between devices: none -> 46.6 us  [collect(): lax.ppermute(line, axis, [(d, (d - have) % ways) for d in range(ways)])]
    dot_general x1, matrix products: 23.9 us -> 32.6 us  [local(): up_proj = jnp.dot(gathered, up_slab, preferred_element_type=jnp.float32)]
where the time goes in v1:
time: 353 us; the launch traced here: 352 us
  waiting for transfers between devices  197 us (56%)
  matrix products  57.7 us (16%)
  blocking collectives  55.7 us (16%)
  other arithmetic  13.8 us (4%)
  between operations  13.5 us (4%)
  local copies, waits for them, and re-layouts  8.66 us (2%)
  starting transfers between devices  6.13 us (2%)
    reduce_scatter x1, waiting for transfers between devices, local(): lax.psum_scatter(partial_sums, 'etp', scatter_dimension=1, tiled=True)  101 us
    all_to_all x1, blocking collectives, local(): lax.all_to_all(outgoing, 'expert', split_axis=0, concat_axis=0, tiled=True)  55.7 us
    all_to_all x1, waiting for transfers between devices, local(): lax.all_to_all(own_cols.reshape(expert_count, capacity, part_width), 'exp...  48.8 us
    ppermute x1, waiting for transfers between devices, collect(): lax.ppermute(line, axis, [(d, (d - have) % ways) for d in range(ways)])  46.6 us
    dot_general x1, matrix products, local(): up_proj = jnp.dot(gathered, up_slab, preferred_element_type=jnp.float32)  32.6 us
    dot_general x1, matrix products, local(): jnp.dot(hidden, down_slab, preferred_element_type=jnp.float32)  24.4 us
    reduce_sum x1, other arithmetic, local(): mixed = jnp.sum(picked * mixing[:, :, None], axis=1)  7.44 us
  transfers between devices with their start and end apart: 3, of which 3 were waited for; matrix products, arithmetic and copies ran while one was open for 0% of the time, Pallas kernels for 0%

profile of v1, /device:TPU:0, one launch (start us, length us, event | category | flops | bytes accessed | tf_op | source)
XLA Modules:
  0.0 352.4 jit_solution(12369411550982560324)
XLA Ops:
  6.5 0.9 copy.18
  7.4 0.1 eq.42
  7.6 0.1 reshape.81
  7.7 1.2 reduce-window.6
  9.0 0.2 slice_reduce_fusion
  9.2 0.2 reduce-window.9
  9.5 0.1 reduce_sum.35
  9.7 0.7 compare_and_fusion
  10.4 0.3 fusion.15
  10.7 0.7 convolution_convert_fusion
  11.4 55.7 %all_to_all.10 = bf16[4,176,1536]{2,1,0:T(8,128)(2,1)S(1)} all-to-all(bf16[4,176,1536]{2,1,0:T(8,128)(2,1)S(1)} %bitcast.43), channel_id=1, replica_groups=mesh['dp'=4,'expert'=4,'etp'=2] {'expert'}, dimensions={0} | all-to-all | bytes 4325376 | tf_op jit(solution)/shard_map/all_to_all | solution.py:51
  67.2 1.5 collective-permute-start
  68.7 46.6 %collective-permute-done = bf16[704,1536]{1,0:T(8,128)(2,1)} collective-permute-done((bf16[704,1536]{1,0:T(8,128)(2,1)S(1)}, bf16[704,1536]{1,0:T(8,128)(2,1)}, u32[]{:S(2)}, u32[]{:S(2)}) %collective-permute-start) | collective-permute-done | bytes 2162720 | tf_op jit(solution)/shard_map/ppermute | solution.py:12
  115.3 32.6 %multiply_convert_fusion.4 = bf16[704,4096]{1,0:T(8,128)(2,1)} fusion(bf16[1,3072,4096]{2,1,0:T(8,128)(2,1)} %param.8, s32[]{:T(128)S(6)} %select_n.37, bf16[704,1536]{1,0:T(8,128)(2,1)S(1)} %bitcast.46, bf16[704,1536]{1,0:T(8,128)(2,1)} %collective-permute-done), kind=kOutput, calls=%fused_computation.5.clone.clone.1 | convolution fusion | flops 17748459520 | bytes 35258372 | tf_op jit(solution)/shard_map/dot_general | solution.py:53
  147.8 24.4 %fusion = f32[704,3072]{1,0:T(8,128)} fusion(bf16[1,4096,3072]{2,1,0:T(8,128)(2,1)} %param.9, bf16[704,4096]{1,0:T(8,128)(2,1)} %multiply_convert_fusion.4), kind=kOutput, calls=%fused_computation.1 | convolution fusion | flops 17716740096 | bytes 39583744 | tf_op jit(solution)/shard_map/dot_general | solution.py:55
  172.3 101.5 %reduce-scatter.2.cloned.1.call-done = f32[704,1536]{1,0:T(8,128)} async-done(((f32[704,3072]{1,0:T(8,128)}), f32[704,1536]{1,0:T(8,128)}) %reduce-scatter.2.cloned.1.call-update) | async-done | bytes 4325392 | tf_op jit(solution)/shard_map/reduce_scatter | solution.py:56
  273.8 3.8 %convert_element_type.32 = bf16[704,1536]{1,0:T(8,128)(2,1)} convert(f32[704,1536]{1,0:T(8,128)} %reduce-scatter.2.cloned.1.call-done) | non-fusion elementwise | flops 1081344 | bytes 6488064 | tf_op jit(solution)/shard_map/convert_element_type | solution.py:56
  277.6 4.6 %all-to-all-start.1 = ((bf16[4,176,1536]{2,1,0:T(8,128)(2,1)}), bf16[4,176,1536]{2,1,0:T(8,128)(2,1)S(1)}, u32[]{:S(2)}, u32[]{:S(2)}) async-start(bf16[4,176,1536]{2,1,0:T(8,128)(2,1)} %bitcast.44), calls=%async_computation.2 | async-start | bytes 4325376 | tf_op jit(solution)/shard_map/all_to_all | solution.py:59
  282.3 0.1 mul.44
  282.5 0.2 copy.21
  282.8 48.8 %all-to-all-done.1 = bf16[4,176,1536]{2,1,0:T(8,128)(2,1)S(1)} async-done(((bf16[4,176,1536]{2,1,0:T(8,128)(2,1)}), bf16[4,176,1536]{2,1,0:T(8,128)(2,1)S(1)}, u32[]{:S(2)}, u32[]{:S(2)}) %all-to-all-start.1) | async-done | bytes 2162720 | tf_op jit(solution)/shard_map/all_to_all | solution.py:59
  331.6 3.0 gather_fusion
  334.6 3.5 gather.7
  338.1 7.4 %multiply_reduce_fusion = bf16[256,1536]{1,0:T(8,128)(2,1)} fusion(bf16[256,2,1536]{2,1,0:T(2,128)(2,1)S(1)} %gather.7, pred[256,2]{1,0:T(8,128)(4,1)S(1)} %copy.21, f32[256,2]{1,0:T(8,128)S(1)} %copy.23), kind=kLoop, calls=%fused_computation.15 | loop fusion | flops 2752512 | bytes 2361856 | tf_op jit(solution)/shard_map/reduce_sum | solution.py:72
  (19 shorter events, 0.5 us)
Async XLA Ops:
  6.5 4.2 %copy-start = (bf16[256,1536]{1,0:T(8,128)(2,1)S(1)}, bf16[256,1536]{1,0:T(8,128)(2,1)}, u32[]{:S(2)}) copy-start(bf16[256,1536]{1,0:T(8,128)(2,1)} %param.5) | copy-start | bytes 2359300
  6.5 267.2 %reduce-scatter.2.cloned.1.call-start = ((), (), s32[]{:S(2)}) async-start(), calls=%async_computation.3 | async-start | bytes 12976128 | tf_op jit(solution)/shard_map/reduce_scatter | solution.py:56
  67.2 48.1 %collective-permute-start = (bf16[704,1536]{1,0:T(8,128)(2,1)S(1)}, bf16[704,1536]{1,0:T(8,128)(2,1)}, u32[]{:S(2)}, u32[]{:S(2)}) collective-permute-start(bf16[704,1536]{1,0:T(8,128)(2,1)S(1)} %bitcast.45), channel_id=1, source_target_pairs={{0,1},{1,0},{2,3},{3,2},{4,5},{5,4},{6,7},{7,6},{8,9},{9,8},{10,11... | collective-permute-start | bytes 6488072 | tf_op jit(solution)/shard_map/ppermute | solution.py:12
  172.3 109.9 %copy-start.2 = (s32[256,2]{0,1:T(2,128)S(1)}, s32[256,2]{0,1:T(2,128)}, u32[]{:S(2)}) copy-start(s32[256,2]{0,1:T(2,128)} %param.6) | copy-start | bytes 6148
  172.3 110.4 %copy-start.3 = (f32[256,2]{0,1:T(2,128)S(1)}, f32[256,2]{0,1:T(2,128)}, u32[]{:S(2)}) copy-start(f32[256,2]{0,1:T(2,128)} %param.7) | copy-start | bytes 6148
  277.6 54.0 %all-to-all-start.1 = ((bf16[4,176,1536]{2,1,0:T(8,128)(2,1)}), bf16[4,176,1536]{2,1,0:T(8,128)(2,1)S(1)}, u32[]{:S(2)}, u32[]{:S(2)}) async-start(bf16[4,176,1536]{2,1,0:T(8,128)(2,1)} %bitcast.44), calls=%async_computation.2 | async-start | bytes 4325376 | tf_op jit(solution)/shard_map/all_to_all | solution.py:59
  331.6 13.9 %copy-start.1 = (bf16[256,1536]{1,0:T(8,128)(2,1)S(1)}, bf16[256,1536]{1,0:T(8,128)(2,1)}, u32[]{:S(2)}) copy-start(bf16[256,1536]{1,0:T(8,128)(2,1)} %param.5) | copy-start | bytes 2359300
Sparse Core Ops, SparseCore 0:
  172.4 101.3 reduce-scatter.1
